TPU v7x, 8 devices: a whole 2x2x1 slice. The times are simulated.
8 devices in a mesh: dp: 2 (over z, y), tp: 4 (over x, core).
Axes of the slice: x: 2, y: 2, z: 1, core: 2. Of those that a mesh axis runs over, the one named last changes fastest.
Arguments:
- hidden: bfloat16 [32, 3, 3072], P('dp'), parts along dimension 0
- draft_ids: int32 [32, 2], P('dp'), parts along dimension 0
- norm_gain: bfloat16 [3072], replicated
- head_w: bfloat16 [3072, 128256], P(None, 'tp')
Outputs:
- output 1: float32 [32, 2], P('dp'), parts along dimension 0
- output 2: float32 [32, 3], P('dp'), parts along dimension 0
- output 3: float32 [32, 3], P('dp'), parts along dimension 0
There are 2 independent parts. A program takes and returns all parts, laid end to end along the dimension named above; an argument that names none is the same for every part.
All inputs are finite; a program needn't handle non-finite values.
Results may differ from a plain program's by a relative error of at most 0.001.
Values sent between devices are 32-bit elements.
A program may use at most 1 GiB of HBM per device.

v0:
```python
import jax
import jax.numpy as jnp
from jax import lax
from jax.sharding import PartitionSpec as P

NORM_EPS = 1e-5


def rms_norm(hidden, norm_gain):
    wide_x = hidden.astype(jnp.float32)
    inv_rms = lax.rsqrt(jnp.mean(wide_x * wide_x, axis=-1, keepdims=True) + NORM_EPS)
    return (wide_x * inv_rms * norm_gain.astype(jnp.float32)).astype(jnp.bfloat16)


def solution(mesh):
    def per_device(hidden, draft_ids, norm_gain, head_w):
        normed = rms_norm(hidden, norm_gain)
        logits = jnp.einsum('btd,dv->btv', normed, head_w, preferred_element_type=jnp.float32)
        gathered = lax.all_gather(logits, 'tp')
        shards = gathered.shape[0]
        shard_cols = gathered.shape[3]
        drafts = draft_ids.shape[1]
        row_max = jnp.max(gathered, axis=(0, 3))
        shifted = gathered - row_max[None, :, :, None]
        exp_vals = jnp.exp(shifted)
        exp_sum = jnp.sum(exp_vals, axis=(0, 3))
        weighted = jnp.sum(exp_vals * shifted, axis=(0, 3))
        log_sum = jnp.log(exp_sum)
        log_norm = row_max + log_sum
        entropy = log_sum - weighted / exp_sum
        col_ids = lax.broadcasted_iota(jnp.int32, (shards, 1, 1, shard_cols), 0) * shard_cols + lax.broadcasted_iota(jnp.int32, (shards, 1, 1, shard_cols), 3)
        picked = jnp.sum(jnp.where(col_ids == draft_ids[None, :, :, None], gathered[:, :, :drafts], 0.0), axis=(0, 3))
        return picked - log_norm[:, :drafts], log_norm, entropy

    specs_in = (P('dp', None, None), P('dp', None), P(None), P(None, 'tp'))
    specs_out = (P('dp', None), P('dp', None), P('dp', None))
    return jax.shard_map(per_device, mesh=mesh, in_specs=specs_in, out_specs=specs_out, check_vma=False)
```

profile of v0, /device:TPU:0, one launch (start us, length us, event | category | flops | bytes accessed | tf_op | source)
XLA Modules:
  0.0 273.2 jit_solution(5341993289006876928)
XLA Ops:
  7.2 0.0 all-gather.3.cloned.1.call-start
  7.2 0.7 convert_element_type.10
  7.9 1.1 fusion.4
  9.0 72.6 %fusion = f32[16,3,32064]{2,0,1:T(8,128)} fusion(bf16[3072,32064]{0,1:T(8,128)(2,1)} %param.7, bf16[16,3,3072]{2,0,1:T(8,128)(2,1)} %param.4, f32[3072]{0:T(1024)S(1)} %convert_element_type.10, f32[16,3]{0,1:T(4,128)S(1)} %add_rsqrt_fusion), kind=kOutput, calls=%fused_computation | convolution fusion | flops 9456648192 | bytes 203464896 | tf_op jit(solution)/shard_map/btd,dv->btv/dot_general | solution.py:18
  81.6 0.0 all-gather.3.cloned.1.call-update
  81.7 0.1 iota_add_fusion
  81.8 0.0 copy-start.1
  81.8 152.8 %all-gather.3.cloned.1.call-done = f32[64,3,32064]{2,0,1:T(8,128)} async-done(((f32[16,3,32064]{2,0,1:T(8,128)}), f32[64,3,32064]{2,0,1:T(8,128)}) %all-gather.3.cloned.1.call-update) | async-done | bytes 24625168 | tf_op jit(solution)/shard_map/all_gather | solution.py:19
  234.7 9.3 %reduce = f32[64,3]{0,1:T(4,128)S(1)} reduce(f32[64,3,32064]{2,0,1:T(8,128)} %all-gather.3.cloned.1.call-done, f32[]{:T(128)} %constant.10.clone.1), dimensions={2}, to_apply=%region_2.0 | reduce | flops 6156096 | bytes 24625924 | tf_op jit(solution)/shard_map/reduce_max | solution.py:23
  243.9 0.1 reshape.32
  244.1 13.0 %fusion.2 = (f32[16,3]{0,1:T(4,128)S(1)}, f32[16,3]{0,1:T(4,128)S(1)}) fusion(f32[4,16,3,32064]{3,1,0,2:T(8,128)} %bitcast.7, f32[16,3]{0,1:T(4,128)S(1)} %reduce_max.9), kind=kLoop, calls=%fused_computation.4 | loop fusion | flops 24625056 | bytes 24625728 | tf_op jit(solution)/shard_map/reduce_sum | solution.py:27
  257.1 0.6 divide_subtract_fusion
  257.7 0.0 copy-done.1
  257.7 0.0 copy-start
  257.7 8.1 %fusion.3 = f32[16,2]{0,1:T(2,128)S(1)} fusion(f32[4,16,3,32064]{3,1,0,2:T(8,128)} %bitcast.8, s32[16,2]{0,1:T(2,128)S(1)} %copy-done.1, s32[4,32064]{1,0:T(4,128)S(1)} %iota_add_fusion), kind=kLoop, calls=%fused_computation.6 | loop fusion | flops 12312544 | bytes 16930048 | tf_op jit(solution)/shard_map/reduce_sum | solution.py:32
  265.8 0.6 slice_subtract_fusion
  266.4 0.0 copy-done
  (3 shorter events, 0.0 us)
Async XLA Ops:
  7.2 227.5 %all-gather.3.cloned.1.call-start = ((), (), s32[]{:S(2)}) async-start(), calls=%async_computation | async-start | bytes 30842880 | tf_op jit(solution)/shard_map/all_gather | solution.py:19
  81.8 175.9 %copy-start.1 = (s32[16,2]{0,1:T(2,128)S(1)}, s32[16,2]{0,1:T(2,128)}, u32[]{:S(2)}) copy-start(s32[16,2]{0,1:T(2,128)} %param.5) | copy-start | bytes 388
  257.7 8.7 %copy-start = (f32[16,3]{0,1:T(4,128)}, f32[16,3]{0,1:T(4,128)S(1)}, u32[]{:S(2)}) copy-start(f32[16,3]{0,1:T(4,128)S(1)} %get-tuple-element.6) | copy-start | bytes 580
Sparse Core Ops, SparseCore 0:
  81.8 152.8 all-gather.2
where the time goes:
time: 274 us; the launch traced here: 273 us
  waiting for transfers between devices  153 us (56%)
  matrix products  72.6 us (26%)
  other arithmetic  33.5 us (12%)
  between operations  14.1 us (5%)
    all_gather x1, waiting for transfers between devices, per_device(): gathered = lax.all_gather(logits, 'tp')  153 us
    dot_general x1, matrix products, per_device(): jnp.einsum('btd,dv->btv', normed, head_w, preferred_element_type=jnp.floa...  72.6 us
    reduce_sum x1, other arithmetic, per_device(): weighted = jnp.sum(exp_vals * shifted, axis=(0, 3))  13 us
    reduce_max x2, other arithmetic, per_device(): row_max = jnp.max(gathered, axis=(0, 3))  9.31 us
    reduce_sum x1, other arithmetic, per_device(): jnp.sum(jnp.where(col_ids == draft_ids[None, :, :, None], gathered[:, :,...  8.08 us
  transfers between devices with their start and end apart: 1, of which 1 were waited for; matrix products, arithmetic and copies ran while one was open for 0% of the time, Pallas kernels for 0%

commit v1 on v0

v1 whole, which is shorter than its diff:
```python
import functools

import jax
import jax.numpy as jnp
from jax import lax
from jax.experimental import pallas as pl
from jax.experimental.pallas import tpu as pltpu
from jax.sharding import PartitionSpec as P

NORM_EPS = 1e-5
DP, TP = 2, 4
LANES = 128
BLOCK = 1024
TAIL = 336
SLOTS = 8
PARTS = 4
MESH = pl.DeviceIdType.MESH
F32 = jnp.float32
LOWEST = float(jnp.finfo(jnp.float32).min)


def fold(m, s, w, m_new):
    d = jnp.maximum(m - m_new, LOWEST)
    a = jnp.exp(d)
    return a * s, a * (w + s * d)


def kernel(cfg, x_hbm, ids_hbm, gain_hbm, w_hbm, logp_ref, norm_ref, ent_ref,
           x_v, gain_v, ids_s, wbuf, nsend, nrecv, n_all, n_t, id_send, id_recv, stat, gath,
           x_sem, gain_sem, ids_sem, w_sem, ns_sem, nr_sem, rs_sem, rr_sem, id_sem, st_send, st_recv):
    seqs, toks, dim, cols, half, full, tails = cfg
    rows = seqs * toks
    part = dim // PARTS
    dp, tp = lax.axis_index("dp"), lax.axis_index("tp")
    core = lax.rem(tp, 2)
    base = dp * half

    x_copy = pltpu.make_async_copy(x_hbm, x_v, x_sem)
    gain_copy = pltpu.make_async_copy(gain_hbm, gain_v, gain_sem)
    ids_copy = pltpu.make_async_copy(ids_hbm, ids_s, ids_sem)
    x_copy.start()
    gain_copy.start()
    ids_copy.start()

    def block_copy(j, slot):
        start = pl.multiple_of(base + j * BLOCK, 32)
        return pltpu.make_async_copy(w_hbm.at[pl.ds(start, BLOCK), :], wbuf.at[slot], w_sem.at[slot])

    tail_slot = full % SLOTS

    def tail_copy(i):
        start = pl.multiple_of(base + full * BLOCK + i * TAIL, 16)
        return pltpu.make_async_copy(w_hbm.at[pl.ds(start, TAIL), :],
                                     wbuf.at[tail_slot, pl.ds(i * TAIL, TAIL), :], w_sem.at[SLOTS + i])

    for j in range(SLOTS):
        block_copy(j, j).start()

    barrier = pltpu.get_barrier_semaphore()
    others = [(a, b) for a in range(DP) for b in range(TP) if (a, b) != (0, 0)]

    def device(a, b):
        return (lax.rem(dp + a, DP), lax.rem(tp + b, TP))

    for a, b in others:
        pl.semaphore_signal(barrier, inc=1, device_id=device(a, b), device_id_type=MESH)

    x_copy.wait()
    gain_copy.wait()
    gain = gain_v[...].astype(F32)
    for t in range(toks):
        x = x_v[t].astype(F32)
        inv = lax.rsqrt(jnp.mean(x * x, axis=-1, keepdims=True) + NORM_EPS)
        n = (x * inv * gain).astype(jnp.bfloat16)
        n_all[pl.ds(t * seqs, seqs), :] = n
        for q in range(PARTS):
            nsend[q, pl.ds(t * seqs, seqs), :] = n[:, q * part:(q + 1) * part].astype(F32)
    n_all[pl.ds(2 * rows, LANES - 2 * rows), :] = jnp.zeros((LANES - 2 * rows, dim), jnp.bfloat16)
    ids_copy.wait()
    lane = lax.broadcasted_iota(jnp.int32, (8, LANES), 1)
    own_ids = jnp.full((8, LANES), -1, jnp.int32)
    for t in range(toks - 1):
        for b in range(seqs):
            own_ids = jnp.where(lane == t * seqs + b, ids_s[t, b], own_ids)
    id_send[...] = own_ids

    pl.semaphore_wait(barrier, len(others))

    mine = PARTS // 2
    sends = []
    for q in range(mine):
        p = core * mine + q
        sends.append(pltpu.make_async_remote_copy(
            nsend.at[p], nrecv.at[p], ns_sem.at[q], nr_sem.at[q], device_id=device(1, 0), device_id_type=MESH))
        sends[-1].start()
    id_copy = pltpu.make_async_remote_copy(
        id_send, id_recv, id_sem.at[0], id_sem.at[1], device_id=device(1, 0), device_id_type=MESH)
    id_copy.start()
    partner = (dp, tp + 1 - 2 * core)
    relays = []
    for q in range(mine):
        sends[q].wait_recv()
        p = core * mine + q
        relays.append(pltpu.make_async_remote_copy(
            nrecv.at[p], nrecv.at[p], rs_sem.at[q], rr_sem.at[q], device_id=partner, device_id_type=MESH))
        relays[-1].start()
    id_copy.wait_recv()
    ids = jnp.where((lane >= rows) & (lane < 2 * rows), pltpu.roll(id_recv[...], rows, 1), own_ids)
    for q in range(mine):
        relays[q].wait_recv()
    for q in range(PARTS):
        n_all[pl.ds(rows, rows), pl.ds(q * part, part)] = nrecv[q].astype(jnp.bfloat16)
    n_t[...] = n_all[...].T

    first = tp * cols + base
    offset = ids - first - lax.broadcasted_iota(jnp.int32, (8, LANES), 0)

    def update(carry, w_block, size, begin):
        m, s, w, picked = carry
        z = jnp.dot(w_block, n_t[...], preferred_element_type=F32).reshape(size // 8, 8, LANES)
        m_new = jnp.maximum(m, jnp.max(z, axis=0))
        s, w = fold(m, s, w, m_new)
        shifted = z - m_new[None]
        e = jnp.exp(shifted)
        s = s + jnp.sum(e, axis=0)
        w = w + jnp.sum(e * shifted, axis=0)
        at = 8 * lax.broadcasted_iota(jnp.int32, (size // 8, 8, LANES), 0)
        picked = picked + jnp.sum(jnp.where((offset - begin)[None] == at, z, 0.0), axis=0)
        return m_new, s, w, picked

    def step(j, carry):
        slot = lax.rem(j, SLOTS)
        block_copy(j, slot).wait()
        carry = update(carry, wbuf[slot], BLOCK, j * BLOCK)

        @pl.when(j + SLOTS < full)
        def _():
            block_copy(j + SLOTS, slot).start()

        @pl.when(j + SLOTS == full)
        def _():
            for i in range(tails):
                tail_copy(i).start()

        return carry

    zero = jnp.zeros((8, LANES), F32)
    carry = lax.fori_loop(0, full, step, (jnp.full((8, LANES), LOWEST, F32), zero, zero, zero))
    for i in range(tails):
        tail_copy(i).wait()
        carry = update(carry, wbuf[tail_slot, pl.ds(i * TAIL, TAIL), :], TAIL, full * BLOCK + i * TAIL)
    m, s, w, picked = carry

    top = jnp.max(m, axis=0, keepdims=True)
    s, w = fold(m, s, w, top)
    stat[0:1, :] = top
    stat[1:2, :] = jnp.sum(s, axis=0, keepdims=True)
    stat[2:3, :] = jnp.sum(w, axis=0, keepdims=True)
    stat[3:4, :] = jnp.sum(picked, axis=0, keepdims=True)
    stat[4:8, :] = jnp.zeros((4, LANES), F32)
    stat_copies = []
    for i, (a, b) in enumerate(others):
        stat_copies.append(pltpu.make_async_remote_copy(
            stat, gath.at[i], st_send.at[i], st_recv.at[i], device_id=device(a, b), device_id_type=MESH))
        stat_copies[-1].start()
    tiles = [stat[...]]
    for i, (a, b) in enumerate(others):
        stat_copies[i].wait_recv()
        tile = gath[i]
        tiles.append(tile if a == 0 else pltpu.roll(tile, LANES - rows, 1))
    top = functools.reduce(jnp.maximum, [t[0:1, :] for t in tiles])
    parts = [fold(t[0:1, :], t[1:2, :], t[2:3, :], top) for t in tiles]
    s = sum(q[0] for q in parts)
    w = sum(q[1] for q in parts)
    picked = sum(t[3:4, :] for t in tiles)
    log_s = jnp.log(s)
    log_norm = top + log_s
    entropy = log_s - w / s
    logp = picked - log_norm
    for t in range(toks):
        shift = (LANES - t * seqs) % LANES
        norm_ref[t:t + 1, :] = pltpu.roll(log_norm, shift, 1)[:, :seqs]
        ent_ref[t:t + 1, :] = pltpu.roll(entropy, shift, 1)[:, :seqs]
        if t < toks - 1:
            logp_ref[t:t + 1, :] = pltpu.roll(logp, shift, 1)[:, :seqs]

    for copy in sends + relays + [id_copy] + stat_copies:
        copy.wait_send()


def solution(mesh):
    def per_device(hidden, draft_ids, norm_gain, head_w):
        seqs, toks, dim = hidden.shape
        cols = head_w.shape[1]
        half = cols // DP
        full = half // BLOCK
        tails = (half - full * BLOCK) // TAIL
        assert half == full * BLOCK + tails * TAIL
        rows = seqs * toks
        cfg = (seqs, toks, dim, cols, half, full, tails)
        any_spec = pl.BlockSpec(memory_space=pl.ANY)
        vmem_spec = pl.BlockSpec(memory_space=pltpu.VMEM)
        dma = pltpu.SemaphoreType.DMA
        mine = PARTS // 2
        logp, norm, ent = pl.pallas_call(
            functools.partial(kernel, cfg),
            out_shape=[jax.ShapeDtypeStruct((toks - 1, seqs), F32),
                       jax.ShapeDtypeStruct((toks, seqs), F32),
                       jax.ShapeDtypeStruct((toks, seqs), F32)],
            in_specs=[any_spec] * 4,
            out_specs=[vmem_spec] * 3,
            scratch_shapes=[
                pltpu.VMEM((toks, seqs, dim), jnp.bfloat16),
                pltpu.VMEM((1, dim), jnp.bfloat16),
                pltpu.SMEM((toks - 1, seqs), jnp.int32),
                pltpu.VMEM((SLOTS, BLOCK, dim), jnp.bfloat16),
                pltpu.VMEM((PARTS, rows, dim // PARTS), F32),
                pltpu.VMEM((PARTS, rows, dim // PARTS), F32),
                pltpu.VMEM((LANES, dim), jnp.bfloat16),
                pltpu.VMEM((dim, LANES), jnp.bfloat16),
                pltpu.VMEM((8, LANES), jnp.int32),
                pltpu.VMEM((8, LANES), jnp.int32),
                pltpu.VMEM((8, LANES), F32),
                pltpu.VMEM((DP * TP - 1, 8, LANES), F32),
                dma, dma, dma, dma((SLOTS + 2,)), dma((mine,)), dma((mine,)), dma((mine,)), dma((mine,)),
                dma((2,)), dma((DP * TP - 1,)), dma((DP * TP - 1,)),
            ],
            compiler_params=pltpu.CompilerParams(
                collective_id=0, has_side_effects=True, vmem_limit_bytes=66_000_000),
        )(hidden.transpose(1, 0, 2), draft_ids.T, norm_gain.reshape(1, dim), head_w.T)
        return logp.T, norm.T, ent.T

    specs_in = (P('dp', None, None), P('dp', None), P(None), P(None, 'tp'))
    specs_out = (P('dp', None), P('dp', None), P('dp', None))
    return jax.shard_map(per_device, mesh=mesh, in_specs=specs_in, out_specs=specs_out, check_vma=False)
```

time: 274 us -> 67.2 us (0.25)
  waiting for transfers between devices: 153 us -> 0 us
  matrix products: 72.6 us -> 0 us
  Pallas kernels: 0 us -> 61.4 us
  other arithmetic: 33.5 us -> 0 us
  between operations: 14.1 us -> 0.64 us
  local copies, waits for them, and re-layouts: 0.1 us -> 4.97 us
    all_gather x1 -> x0, waiting for transfers between devices: 153 us -> none  [per_device(): gathered = lax.all_gather(logits, 'tp')]
    dot_general x1 -> x0, matrix products: 72.6 us -> none  [per_device(): jnp.einsum('btd,dv->btv', normed, head_w, preferred_element_type=jnp.floa...]
    pallas_call x0 -> x1, Pallas kernels: none -> 61.4 us  [per_device(): pl.pallas_call(functools.partial(kernel, cfg), out_shape=[jax.ShapeDtypeS...]
    reduce_sum x3 -> x0, other arithmetic: 22.2 us -> none  [the longest x1 13 us: per_device(): weighted = jnp.sum(exp_vals * shifted, axis=(0, 3))]
    reduce_max x2 -> x0, other arithmetic: 9.31 us -> none  [per_device(): row_max = jnp.max(gathered, axis=(0, 3))]
    unnamed x4 -> x3, local copies, waits for them, and re-layouts: 0.01 us -> 3.67 us
  transfers between devices with their start and end apart: 1 -> 0, of which waited for: 1 -> 0; matrix products, arithmetic and copies ran while one was open for 0% -> 0% of each run, Pallas kernels for 0% -> 0%
where the time goes in v1:
time: 67.2 us; the launch traced here: 67 us
  Pallas kernels  61.4 us (91%)
  local copies, waits for them, and re-layouts  4.97 us (7%)
    pallas_call x1, Pallas kernels, per_device(): pl.pallas_call(functools.partial(kernel, cfg), out_shape=[jax.ShapeDtypeS...  61.4 us
    unnamed x3, local copies, waits for them, and re-layouts  3.67 us

profile of v1, /device:TPU:0, one launch (start us, length us, event | category | flops | bytes accessed | tf_op | source)
XLA Modules:
  0.0 67.0 jit_solution(3745583223166490220)
XLA Ops:
  0.6 1.3 %reshape.9.gain_hbm = bf16[1,3072]{1,0:T(2,128)(2,1)} reshape(bf16[3072]{0:T(1024)(128)(2,1)} %param.6) | data formatting | bytes 12288 | tf_op jit(solution)/shard_map/reshape | solution.py:230
  1.9 61.4 %shard_map.67 = (f32[2,16]{1,0:T(2,128)}, f32[3,16]{1,0:T(4,128)}, f32[3,16]{1,0:T(4,128)}) custom-call(bf16[3,16,3072]{2,1,0:T(8,128)(2,1)} %bitcast.6, s32[2,16]{1,0:T(2,128)} %bitcast.9, bf16[1,3072]{1,0:T(2,128)(2,1)} %reshape.9.gain_hbm, bf16[32064,3072]{1,0:T(8,128)(2,1)} %bitcast.2.w_hbm), custom_call_target="tpu_custom_call" | custom-call | tf_op jit(solution)/shard_map/pallas_call | solution.py:205
  63.3 1.2 %copy.10 = f32[16,2]{0,1:T(2,128)} copy(f32[16,2]{0,1:T(2,128)} %bitcast.10) | data formatting | bytes 256
  64.5 1.2 %copy.11 = f32[16,3]{0,1:T(4,128)} copy(f32[16,3]{0,1:T(4,128)} %bitcast.8) | data formatting | bytes 384
  65.8 1.2 %copy.12 = f32[16,3]{0,1:T(4,128)} copy(f32[16,3]{0,1:T(4,128)} %bitcast.7) | data formatting | bytes 384
